TPU v7x, 32 devices: a whole 2x2x4 slice. The times are simulated.
32 devices in a mesh: ep: 32 (over z, y, x, core).
Axes of the slice: x: 2, y: 2, z: 4, core: 2. Of those that a mesh axis runs over, the one named last changes fastest.
Arguments:
- tokens: bfloat16 [192, 1024, 1024], P('ep')
- loss_weight: bfloat16 [192, 1024, 1024], P('ep')
- w_gate: bfloat16 [1024, 32], replicated
- w_in: bfloat16 [32, 1024, 512], P('ep')
- w_out: bfloat16 [32, 512, 1024], P('ep')
- first_expert: int32 [192, 1024], P('ep')
- second_expert: int32 [192, 1024], P('ep')
- keep_second: int32 [192, 1024], P('ep')
Outputs:
- output 1: float32 [], replicated
- output 2: bfloat16 [192, 1024, 1024], P('ep')
- output 3: bfloat16 [32, 1024, 512], P('ep')
- output 4: bfloat16 [32, 512, 1024], P('ep')
- output 5: float32 [1024, 32], replicated
All inputs are finite; a program needn't handle non-finite values.
Results may differ from a plain program's by a relative error of at most 0.00968334.
Values are sent between devices in bfloat16 or wider.
A program may use at most 1 GiB of HBM per device.

v0:
```python
import jax
import jax.numpy as jnp
from jax import lax
from jax.experimental import pallas as pl
from jax.experimental.pallas import tpu as pltpu
from jax.sharding import PartitionSpec as P


ALPHA = 0.01
F32 = jnp.float32
BF16 = jnp.bfloat16
I32 = jnp.int32
PLANE = 8
CHUNKS = 2
VMEM_LIMIT = 60 * 1024 * 1024


def route_slots(first_ids, second_ids, keep_ids, experts, cap_rows):
    seq_len = first_ids.shape[1]
    expert_ids = jnp.arange(experts, dtype=I32)
    first_hot = (first_ids[..., None] == expert_ids).astype(BF16)
    second_hot = (second_ids[..., None] == expert_ids).astype(BF16)
    second_kept = second_hot * keep_ids.astype(BF16)[..., None]
    seq_ids = jnp.arange(seq_len, dtype=I32)
    earlier = (seq_ids[:, None] > seq_ids[None, :]).astype(BF16)
    before_first = jnp.einsum('st,gte->gse', earlier, first_hot, preferred_element_type=F32)
    before_second = jnp.einsum('st,gte->gse', earlier, second_kept, preferred_element_type=F32)
    first_count = jnp.sum(first_hot, axis=1, dtype=F32)
    pos_first = jnp.sum(before_first * first_hot, axis=-1).astype(I32)
    pos_second = jnp.sum((before_second + first_count[:, None, :]) * second_hot, axis=-1).astype(I32)
    pos_first = jnp.where(pos_first < cap_rows, pos_first, -1)
    pos_second = jnp.where((keep_ids > 0) & (pos_second < cap_rows), pos_second, -1)
    return first_hot, second_hot, first_count, pos_first, pos_second


def dispatch_kernel(first_ref, second_ref, rows_ref, out_ref):
    peers, parts, _, cap_rows, hidden = out_ref.shape
    per_peer = parts * cap_rows
    rows = rows_ref[0]

    @pl.loop(0, peers, step=2)
    def _(peer):
        slot = lax.broadcasted_iota(I32, (2 * per_peer, rows.shape[0]), 0) + peer * per_peer
        hit = (slot == first_ref[0]) | (slot == second_ref[0])
        table = jnp.where(hit, 1.0, 0.0).astype(BF16)
        picked = jnp.dot(table, rows, preferred_element_type=F32).astype(BF16)
        out_ref[pl.ds(peer, 2)] = picked.reshape(2, parts, 1, cap_rows, hidden)


def dispatch(first_slot, second_slot, rows, parts, cap_rows):
    groups, seq_len, hidden = rows.shape
    slots = PLANE * parts * cap_rows
    return pl.pallas_call(
        dispatch_kernel,
        grid=(groups,),
        in_specs=[
            pl.BlockSpec((1, 1, seq_len), lambda g: (g, 0, 0)),
            pl.BlockSpec((1, 1, seq_len), lambda g: (g, 0, 0)),
            pl.BlockSpec((1, seq_len, hidden), lambda g: (g, 0, 0)),
        ],
        out_specs=pl.BlockSpec((PLANE, parts, 1, cap_rows, hidden), lambda g: (0, 0, g, 0, 0)),
        out_shape=jax.ShapeDtypeStruct((PLANE, parts, groups, cap_rows, hidden), BF16),
        compiler_params=pltpu.CompilerParams(vmem_limit_bytes=VMEM_LIMIT),
        cost_estimate=pl.CostEstimate(flops=2 * groups * slots * seq_len * hidden, bytes_accessed=4 * groups * seq_len * hidden, transcendentals=0),
        name='dispatch_rows',
    )(first_slot[:, None, :], second_slot[:, None, :], rows)


def dot_nn(a, b):
    return jnp.dot(a, b, preferred_element_type=F32)


def dot_nt(a, b):
    return lax.dot_general(a, b, (((1,), (1,)), ((), ())), preferred_element_type=F32)


def dot_tn(a, b):
    return lax.dot_general(a, b, (((0,), (0,)), ((), ())), preferred_element_type=F32)


def expert_kernel(x_ref, r_ref, norm_ref, w_in_ref, w_out_ref, *refs):
    slots_ref, dots_ref, d_in_ref, d_out_ref = refs[-4:]
    first = pl.program_id(1) == 0
    _, _, groups, cap_rows, hidden = x_ref.shape
    x = x_ref[...].reshape(groups * cap_rows, hidden)
    r = r_ref[...].reshape(groups * cap_rows, hidden)
    w_in = w_in_ref[0]
    w_out = w_out_ref[0]
    r_wide = r.astype(F32)
    grad_y = (r_wide * norm_ref[0, 0]).astype(BF16)
    pre = dot_nn(x, w_in)
    scale = 0.7978845608028654
    square = pre * pre
    tanh = jnp.tanh(scale * (pre + 0.044715 * (square * pre)))
    half = 0.5 * (1.0 + tanh)
    act = (pre * half).astype(BF16)
    slope = half + 0.5 * pre * (1.0 - tanh * tanh) * (scale * (1.0 + 3.0 * 0.044715 * square))
    grad_act = dot_nt(grad_y, w_out).astype(BF16).astype(F32)
    grad_pre = (grad_act * slope).astype(BF16)
    slots_ref[...] = dot_nt(grad_pre, w_in).astype(BF16).reshape(slots_ref.shape)
    out = dot_nn(act, w_out).astype(BF16).astype(F32)
    dots_ref[0, 0] = jnp.sum(out * r_wide, axis=1, keepdims=True)
    d_out = dot_tn(act, grad_y)
    d_in = dot_tn(x, grad_pre)

    @pl.when(first)
    def _():
        d_out_ref[0] = d_out
        d_in_ref[0] = d_in

    @pl.when(jnp.logical_not(first))
    def _():
        d_out_ref[0] += d_out
        d_in_ref[0] += d_in


def expert_part(part, parts, x_slots, r_slots, norms, w_in, w_out, earlier):
    peers, _, groups, cap_rows, hidden = x_slots.shape
    _, _, ff_dim = w_in.shape
    rows = groups * cap_rows
    block = pl.BlockSpec((1, 1, groups, cap_rows, hidden), lambda e, s: (s, e, 0, 0, 0))
    column = pl.BlockSpec((1, 1, rows, 1), lambda e, s: (s, e, 0, 0))
    norm_column = pl.BlockSpec((1, 1, rows, 1), lambda e, s: (s, parts * part + e, 0, 0))
    in_block = pl.BlockSpec((1, hidden, ff_dim), lambda e, s: (parts * part + e, 0, 0))
    out_block = pl.BlockSpec((1, ff_dim, hidden), lambda e, s: (parts * part + e, 0, 0))
    return pl.pallas_call(
        expert_kernel,
        grid=(parts, peers),
        in_specs=[block, block, norm_column, in_block, out_block] + [pl.BlockSpec(memory_space=pl.ANY)] * len(earlier),
        out_specs=[block, column, in_block, out_block],
        out_shape=[
            jax.ShapeDtypeStruct(x_slots.shape, BF16),
            jax.ShapeDtypeStruct((peers, parts, rows, 1), F32),
            jax.ShapeDtypeStruct(w_in.shape, F32),
            jax.ShapeDtypeStruct(w_out.shape, F32),
        ],
        input_output_aliases={5 + i: 2 + i for i in range(len(earlier))},
        compiler_params=pltpu.CompilerParams(vmem_limit_bytes=VMEM_LIMIT, dimension_semantics=('arbitrary', 'arbitrary')),
        cost_estimate=pl.CostEstimate(flops=12 * parts * peers * rows * hidden * ff_dim, bytes_accessed=6 * parts * peers * rows * hidden, transcendentals=parts * peers * rows * ff_dim),
        name='expert_part',
    )(x_slots, r_slots, norms, w_in, w_out, *earlier)


def gathered(first_ref, second_ref, slots_ref, acc):
    _, rows, _ = first_ref.shape
    slots = slots_ref[...].reshape(-1, slots_ref.shape[-1])
    slot = lax.broadcasted_iota(I32, (rows, slots.shape[0]), 1)
    hit = (slot == first_ref[0]) | (slot == second_ref[0])
    return acc + dot_nn(jnp.where(hit, 1.0, 0.0).astype(BF16), slots)


def combine_start_kernel(first_ref, second_ref, slots_ref, r_ref, logit_ref, gate_ref, out_ref):
    acc = r_ref[0].astype(F32) + dot_nn(logit_ref[0], gate_ref[...])
    out_ref[0] = gathered(first_ref, second_ref, slots_ref, acc)


def combine_more_kernel(first_ref, second_ref, slots_ref, acc_ref, out_ref):
    out_ref[0] = gathered(first_ref, second_ref, slots_ref, acc_ref[0]).astype(out_ref.dtype)


def combine(first_slot, second_slot, slots, extra, out_type):
    peers, parts, groups, cap_rows, hidden = slots.shape
    seq_len = first_slot.shape[1]
    tile = 256
    column = pl.BlockSpec((1, tile, 1), lambda g, t: (g, t, 0))
    wide = pl.BlockSpec((1, tile, hidden), lambda g, t: (g, t, 0))
    block = pl.BlockSpec((peers, parts, 1, cap_rows, hidden), lambda g, t: (0, 0, g, 0, 0))
    if len(extra) == 1:
        kernel, extra_specs = combine_more_kernel, [wide]
    else:
        experts = extra[1].shape[-1]
        kernel = combine_start_kernel
        extra_specs = [wide, pl.BlockSpec((1, tile, experts), lambda g, t: (g, t, 0)), pl.BlockSpec((experts, hidden), lambda g, t: (0, 0))]
    return pl.pallas_call(
        kernel,
        grid=(groups, seq_len // tile),
        in_specs=[column, column, block] + extra_specs,
        out_specs=wide,
        out_shape=jax.ShapeDtypeStruct((groups, seq_len, hidden), out_type),
        compiler_params=pltpu.CompilerParams(vmem_limit_bytes=VMEM_LIMIT),
        cost_estimate=pl.CostEstimate(flops=2 * groups * seq_len * peers * parts * cap_rows * hidden, bytes_accessed=10 * groups * seq_len * hidden, transcendentals=0),
        name='combine_rows',
    )(first_slot[..., None], second_slot[..., None], slots, *extra)


def after(value, *others):
    return lax.optimization_barrier((value,) + others)[0]


def solution(mesh):
    ep_size = mesh.shape['ep']
    planes = ep_size // PLANE
    plane_groups = [[z * PLANE + p for p in range(PLANE)] for z in range(planes)]
    line_groups = [[z * PLANE + p for z in range(planes)] for p in range(PLANE)]

    def swap(value):
        return lax.all_to_all(value, 'ep', 0, 0, axis_index_groups=plane_groups, tiled=True)

    def layer(x_loc, r_loc, w_gate, w_in_loc, w_out_loc, first_ids, second_ids, keep_ids):
        local_groups, seq_len, hidden = x_loc.shape
        experts = w_gate.shape[1]
        cap_rows = 2 * seq_len // experts
        tokens_all = local_groups * ep_size * seq_len
        numel = tokens_all * hidden
        parts = planes // CHUNKS

        w_in = lax.all_gather(w_in_loc, 'ep', axis=0, axis_index_groups=line_groups, tiled=True)
        w_out = lax.all_gather(w_out_loc, 'ep', axis=0, axis_index_groups=line_groups, tiled=True)

        first_hot, second_hot, first_count, pos_first, pos_second = route_slots(first_ids, second_ids, keep_ids, experts, cap_rows)

        def part_slot(ids, pos, part):
            z, peer = ids // PLANE, ids % PLANE
            here = (pos >= 0) & (z // parts == part)
            return jnp.where(here, (peer * parts + z % parts) * cap_rows + pos, -1)

        slots = [(part_slot(first_ids, pos_first, c), part_slot(second_ids, pos_second, c)) for c in range(CHUNKS)]

        def send(rows, part):
            return dispatch(*slots[part], rows, parts, cap_rows)

        sent_x = [send(x_loc, 0)]
        x_late = after(x_loc, sent_x[0])
        logits = jnp.einsum('gsh,he->gse', x_late, w_gate, preferred_element_type=F32)
        router_prob = jax.nn.softmax(logits, axis=-1)
        gate_first = jnp.sum(router_prob * first_hot, axis=-1)
        gate_second = jnp.sum(router_prob * second_hot, axis=-1)
        gate_sum = gate_first + gate_second
        norm_first = (gate_first / gate_sum).astype(BF16)
        norm_second = (gate_second / gate_sum).astype(BF16)
        slot_ids = jnp.arange(cap_rows, dtype=I32)
        place_first = (pos_first[..., None] == slot_ids).astype(BF16)
        place_second = (pos_second[..., None] == slot_ids).astype(BF16)
        norm_slots = (jnp.einsum('gse,gsc->gec', first_hot * norm_first[..., None], place_first, preferred_element_type=F32)
                      + jnp.einsum('gse,gsc->gec', second_hot * norm_second[..., None], place_second, preferred_element_type=F32))
        norm_slots = norm_slots.astype(BF16).reshape(local_groups, planes, PLANE, cap_rows).transpose(2, 1, 0, 3).reshape(PLANE, planes, local_groups * cap_rows)

        sent_r = [send(r_loc, 0)]
        got_x = [swap(sent_x[0])]
        counts = jnp.sum(first_count, axis=0)
        counts = jnp.zeros((PLANE, 1, local_groups * cap_rows), F32).at[:, :, :experts].set(counts)
        note = jnp.tile(jnp.concatenate([norm_slots.astype(F32), counts], axis=1), (planes, 1, 1))
        note = lax.all_to_all(after(note, got_x[0], sent_r[0]), 'ep', 0, 0, tiled=True)
        frac_first = jnp.sum(note[:, planes, :experts], axis=0) / tokens_all
        got_r = [swap(after(sent_r[0], note))]
        norms = lax.dynamic_slice_in_dim(note, lax.axis_index('ep') // PLANE * PLANE, PLANE, 0)[:, :planes, :, None]
        for c in range(1, CHUNKS):
            sent_x.append(send(x_late, c))
            got_x.append(swap(after(sent_x[c], got_r[c - 1])))
            sent_r.append(send(after(r_loc, sent_r[c - 1]), c))
            got_r.append(swap(after(sent_r[c], got_x[c])))
        grads = ()
        grad_slots = []
        dots = []
        for c in range(CHUNKS):
            out_slots, out_dots, *grads = expert_part(c, parts, got_x[c], got_r[c], norms, w_in, w_out, grads)
            grad_slots.append(out_slots)
            dots.append(out_dots)
        grad_w_in = lax.psum_scatter(grads[0], 'ep', scatter_dimension=0, axis_index_groups=line_groups, tiled=True).astype(BF16)
        grad_w_out = lax.psum_scatter(grads[1], 'ep', scatter_dimension=0, axis_index_groups=line_groups, tiled=True).astype(BF16)
        dots = jnp.concatenate([d[..., 0] for d in dots], axis=1)
        moe_sum = jnp.sum(dots * norms[..., 0])

        back = [swap(after(grad_slots[0], got_r[-1]))]
        dots_back = swap(after(dots.astype(BF16), back[0]))
        for c in range(1, CHUNKS):
            back.append(swap(after(grad_slots[c], dots_back if c == 1 else back[c - 1])))
        dots_back = dots_back.reshape(PLANE, planes, local_groups, cap_rows).transpose(2, 1, 0, 3).reshape(local_groups, experts, cap_rows)

        grad_norm_first = jnp.sum(jnp.einsum('gse,gec->gsc', first_hot, dots_back, preferred_element_type=F32) * place_first, axis=-1)
        grad_norm_second = jnp.sum(jnp.einsum('gse,gec->gsc', second_hot, dots_back, preferred_element_type=F32) * place_second, axis=-1)
        gate_sq = gate_sum * gate_sum
        grad_gate_first = (grad_norm_first - grad_norm_second) * gate_second / gate_sq
        grad_gate_second = (grad_norm_second - grad_norm_first) * gate_first / gate_sq
        grad_prob = grad_gate_first[..., None] * first_hot + grad_gate_second[..., None] * second_hot + (ALPHA * hidden * experts) * frac_first
        grad_logits = router_prob * (grad_prob - jnp.sum(router_prob * grad_prob, axis=-1, keepdims=True))
        grad_logits_bf = lax.optimization_barrier(grad_logits.astype(BF16))
        grad_x = combine(*slots[0], back[0], (r_loc, grad_logits_bf, w_gate.T), F32 if CHUNKS > 1 else BF16)
        for c in range(1, CHUNKS):
            grad_x = combine(*slots[c], back[c], (grad_x,), BF16 if c == CHUNKS - 1 else F32)
        grad_gate_w = jnp.einsum('gsh,gse->he', x_loc, grad_logits_bf, preferred_element_type=F32)

        dot_sum = jnp.einsum('gsh,gsh->', x_late, r_loc, preferred_element_type=F32) + moe_sum
        local_stats = jnp.concatenate([jnp.sum(router_prob, axis=(0, 1)), dot_sum[None]])
        rows = hidden * experts // ep_size // 128
        own = grad_gate_w.reshape(ep_size, rows, 128)
        shared = jnp.zeros((8, 128), F32).at[0, :experts + 1].set(local_stats)
        packed = jnp.concatenate([own, jnp.broadcast_to(shared, (ep_size, 8, 128))], axis=1)
        packed = lax.all_to_all(after(packed, back[-1]), 'ep', 0, 0, tiled=True)
        total = jnp.sum(packed, axis=0)
        grad_gate_w = lax.all_gather(total[:rows], 'ep', axis=0, tiled=True).reshape(hidden, experts)
        global_stats = total[rows]
        mean_prob = global_stats[:experts] / tokens_all
        loss_value = global_stats[experts] / numel + ALPHA * experts * jnp.sum(frac_first * mean_prob)
        return loss_value, grad_x, grad_w_in, grad_w_out, grad_gate_w

    row_spec = P('ep', None, None)
    id_spec = P('ep', None)
    return jax.shard_map(layer, mesh=mesh, in_specs=(row_spec, row_spec, P(None, None), row_spec, row_spec, id_spec, id_spec, id_spec), out_specs=(P(), row_spec, row_spec, row_spec, P(None, None)), check_vma=False)
```

profile of v0, /device:TPU:0, one launch (start us, length us, event | category | flops | bytes accessed | tf_op | source)
XLA Modules:
  0.0 1095.1 jit_solution(15591617063938563092)
XLA Ops:
  7.2 4.0 fusion.12
  11.2 1.1 convert_reduce_fusion.1
  12.4 0.7 fusion.94
  13.1 0.7 fusion.98
  13.8 0.6 copy.156.first_ref
  14.4 4.1 fusion.8
  18.5 0.7 fusion.96
  19.1 0.7 and_select_fusion
  19.8 0.6 copy.157.second_ref
  20.4 21.3 %dispatch_rows.4 = bf16[8,2,6,64,1024]{4,3,2,1,0:T(8,128)(2,1)} custom-call(s32[6,1,1024]{2,1,0:T(1,128)} %copy.156.first_ref, s32[6,1,1024]{2,1,0:T(1,128)} %copy.157.second_ref, bf16[6,1024,1024]{2,1,0:T(8,128)(2,1)} %rows_ref.4), custom_call_target="tpu_custom_call" | custom-call | flops 12884901888 | bytes 25165824 | tf_op jit(solution)/shard_map/dispatch_rows/pallas_call | solution.py:53
  41.7 5.5 all-to-all-start
  47.2 9.2 fusion.109
  56.5 2.0 copy.158
  58.4 38.7 %fusion.106 = (f32[32]{0:T(128)}, f32[6,1024]{1,0:T(8,128)S(1)}, f32[6,1024]{1,0:T(8,128)S(1)}, f32[32]{0:T(128)S(1)}, f32[6,1024,32]{2,1,0:T(8,128)}) fusion(s32[6,1024]{1,0:T(8,128)S(1)} %copy-done.13, s32[6,1024]{1,0:T(8,128)S(1)} %copy-done.6, f32[6,1024,32]{2,1,0:T(8,128)S(1)} %copy.158, f32[6,1024]{1,0:T(8,128)S(1)} %get-tuple-element.111), kind=kOutput, calls=%fused_computation.153 | output fusion | flops 2942943 | bytes 1696000 | tf_op jit(solution)/shard_map/div | solution.py:225
  97.2 3.5 fusion.31
  100.7 3.5 fusion.59
  104.4 21.3 %dispatch_rows.5 = bf16[8,2,6,64,1024]{4,3,2,1,0:T(8,128)(2,1)} custom-call(s32[6,1,1024]{2,1,0:T(1,128)} %copy.156.first_ref, s32[6,1,1024]{2,1,0:T(1,128)} %copy.157.second_ref, bf16[6,1024,1024]{2,1,0:T(8,128)(2,1)} %r_ref.1), custom_call_target="tpu_custom_call" | custom-call | flops 12884901888 | bytes 25165824 | tf_op jit(solution)/shard_map/dispatch_rows/pallas_call | solution.py:53
  125.7 61.2 %all-to-all-done.x_ref = bf16[8,2,6,64,1024]{4,3,2,1,0:T(8,128)(2,1)} async-done(((bf16[8,2,6,64,1024]{4,3,2,1,0:T(8,128)(2,1)}), bf16[8,2,6,64,1024]{4,3,2,1,0:T(8,128)(2,1)}, u32[]{:S(2)}, u32[]{:S(2)}) %all-to-all-start) | async-done | bytes 12582944 | tf_op jit(solution)/shard_map/all_to_all | solution.py:197
  186.9 17.8 %all_to_all.45 = f32[32,5,384]{2,1,0:T(8,128)S(1)} all-to-all(f32[32,5,384]{2,1,0:T(8,128)S(1)} %bitcast.76), channel_id=1, replica_groups=mesh['ep'=32] {'ep'}, dimensions={0} | all-to-all | bytes 491520 | tf_op jit(solution)/shard_map/all_to_all | solution.py:243
  204.7 5.5 all-to-all-start.2
  210.3 0.6 broadcast_in_dim.36.second_ref
  210.9 0.6 copy.168.first_ref
  211.6 21.3 %dispatch_rows.6 = bf16[8,2,6,64,1024]{4,3,2,1,0:T(8,128)(2,1)} custom-call(s32[6,1,1024]{2,1,0:T(1,128)} %copy.168.first_ref, s32[6,1,1024]{2,1,0:T(1,128)} %broadcast_in_dim.36.second_ref, bf16[6,1024,1024]{2,1,0:T(8,128)(2,1)} %rows_ref.4), custom_call_target="tpu_custom_call" | custom-call | flops 12884901888 | bytes 25165824 | tf_op jit(solution)/shard_map/dispatch_rows/pallas_call | solution.py:53
  232.9 116.4 %all-to-all-done.2.r_ref = bf16[8,2,6,64,1024]{4,3,2,1,0:T(8,128)(2,1)} async-done(((bf16[8,2,6,64,1024]{4,3,2,1,0:T(8,128)(2,1)}), bf16[8,2,6,64,1024]{4,3,2,1,0:T(8,128)(2,1)}, u32[]{:S(2)}, u32[]{:S(2)}) %all-to-all-start.2) | async-done | bytes 12582944 | tf_op jit(solution)/shard_map/all_to_all | solution.py:197
  349.3 5.4 all-to-all-start.3
  354.7 0.2 all-gather.3.cloned.1.call-start
  354.9 0.5 all-gather.3.cloned.1.call-update
  355.4 21.4 %dispatch_rows.7 = bf16[8,2,6,64,1024]{4,3,2,1,0:T(8,128)(2,1)} custom-call(s32[6,1,1024]{2,1,0:T(1,128)} %copy.168.first_ref, s32[6,1,1024]{2,1,0:T(1,128)} %broadcast_in_dim.36.second_ref, bf16[6,1024,1024]{2,1,0:T(8,128)(2,1)} %r_ref.1), custom_call_target="tpu_custom_call" | custom-call | flops 12884901888 | bytes 25165824 | tf_op jit(solution)/shard_map/dispatch_rows/pallas_call | solution.py:53
  376.8 116.9 %all-to-all-done.3.x_ref = bf16[8,2,6,64,1024]{4,3,2,1,0:T(8,128)(2,1)} async-done(((bf16[8,2,6,64,1024]{4,3,2,1,0:T(8,128)(2,1)}), bf16[8,2,6,64,1024]{4,3,2,1,0:T(8,128)(2,1)}, u32[]{:S(2)}, u32[]{:S(2)}) %all-to-all-start.3) | async-done | bytes 12582944 | tf_op jit(solution)/shard_map/all_to_all | solution.py:197
  493.6 5.3 all-to-all-start.4
  499.0 0.7 all-gather.5.cloned.1.call-update
  499.8 0.6 copy-done.2
  500.4 3.9 copy.166.norm_ref
  504.4 76.8 %all-gather.5.cloned.1.call-done.w_out_ref = bf16[4,512,1024]{2,1,0:T(8,128)(2,1)} async-done(((bf16[1,512,1024]{2,1,0:T(8,128)(2,1)}), bf16[4,512,1024]{2,1,0:T(8,128)(2,1)}) %all-gather.5.cloned.1.call-update) | async-done | bytes 4194320 | tf_op jit(solution)/shard_map/all_gather | solution.py:208
  581.2 63.0 %expert_part.2 = (bf16[8,2,6,64,1024]{4,3,2,1,0:T(8,128)(2,1)}, f32[8,2,384,1]{3,2,1,0:T(8,128)}, f32[4,1024,512]{2,1,0:T(8,128)}, f32[4,512,1024]{2,1,0:T(8,128)}) custom-call(bf16[8,2,6,64,1024]{4,3,2,1,0:T(8,128)(2,1)} %all-to-all-done.x_ref, bf16[8,2,6,64,1024]{4,3,2,1,0:T(8,128)(2,1)} %all-to-all-done.2.r_ref, f32[8,4,384,1]{3,2,1,0:T(8,128)} %copy.166.norm_ref, ...), custom_call_target="tpu_custom_call" | custom-call | flops 38654705664 | bytes 37748736 | tf_op jit(solution)/shard_map/expert_part/pallas_call | solution.py:126
  644.2 63.1 %expert_part.3 = (bf16[8,2,6,64,1024]{4,3,2,1,0:T(8,128)(2,1)}, f32[8,2,384,1]{3,2,1,0:T(8,128)}, f32[4,1024,512]{2,1,0:T(8,128)}, f32[4,512,1024]{2,1,0:T(8,128)}) custom-call(bf16[8,2,6,64,1024]{4,3,2,1,0:T(8,128)(2,1)} %all-to-all-done.3.x_ref, bf16[8,2,6,64,1024]{4,3,2,1,0:T(8,128)(2,1)} %all-to-all-done.4.r_ref, ...), custom_call_target="tpu_custom_call", output_to_operand_aliasing={{2}: (5, {}), {3}: (6, {})} | custom-call | flops 38654705664 | bytes 37748736 | tf_op jit(solution)/shard_map/expert_part/pallas_call | solution.py:126
  707.3 5.3 all-to-all-start.5
  712.7 0.5 reduce-scatter.5.cloned.1.call-update
  713.3 1.4 copy-done.1
  714.7 1.8 copy.167
  716.4 2.4 copy.171
  718.8 132.9 %all-to-all-done.5.slots_ref = bf16[8,2,6,64,1024]{4,3,2,1,0:T(8,128)(2,1)} async-done(((bf16[8,2,6,64,1024]{4,3,2,1,0:T(8,128)(2,1)}), bf16[8,2,6,64,1024]{4,3,2,1,0:T(8,128)(2,1)}, u32[]{:S(2)}, u32[]{:S(2)}) %all-to-all-start.5) | async-done | bytes 12582944 | tf_op jit(solution)/shard_map/all_to_all | solution.py:197
  851.7 7.2 all_to_all.46
  858.8 5.7 all-to-all-start.7
  864.6 2.3 copy.180.second_ref
  866.8 2.2 copy.179.first_ref
  869.0 2.2 copy.182.second_ref
  871.3 2.2 copy.181.first_ref
  873.5 12.4 %fusion.2 = f32[]{:T(128)} fusion(bf16[6,1024,1024]{2,1,0:T(8,128)(2,1)} %r_ref.1, bf16[6,1024,1024]{2,1,0:T(8,128)(2,1)} %rows_ref.4), kind=kLoop, calls=%fused_computation.3 | loop fusion | flops 25165824 | bytes 25165828 | tf_op jit(solution)/shard_map/gsh,gsh->/dot_general | solution.py:283
  885.9 0.6 multiply_reduce_fusion.3
  888.1 2.0 multiply_reduce_fusion.1
  890.1 2.0 multiply_reduce_fusion.2
  892.1 62.2 %multiply_convert_fusion.logit_ref = bf16[6,1024,32]{2,1,0:T(8,128)(2,1)S(1)} fusion(f32[6,1024,32]{2,1,0:T(8,128)} %get-tuple-element.113, f32[32]{0:T(128)S(1)} %broadcast_multiply_fusion, f32[6,1024]{1,0:T(8,128)S(1)} %get-tuple-element.102, f32[6,1024]{1,0:T(8,128)S(1)} %get-tuple-element.101, s32[6,1024]{1,0:T(8,128)S(1)} %copy-done.14, ...), kind=kOutput, calls=%fused_computation.22 | output fusion | flops 4724767 | bytes 1278080 | tf_op jit(solution)/shard_map/sub | solution.py:276
  954.3 7.5 convolution_bitcast_fusion
  962.2 0.7 pad_maximum_fusion
  963.0 35.8 %combine_rows.2.acc_ref = f32[6,1024,1024]{2,1,0:T(8,128)} custom-call(s32[6,1024,1]{2,1,0:T(8,128)} %copy.179.first_ref, s32[6,1024,1]{2,1,0:T(8,128)} %copy.180.second_ref, bf16[8,2,6,64,1024]{4,3,2,1,0:T(8,128)(2,1)} %all-to-all-done.5.slots_ref, bf16[6,1024,1024]{2,1,0:T(8,128)(2,1)} %r_ref.1, bf16[6,1024,32]{2,1,0:T(8,128)(2,1)} %copy-done, ...), custom_call_target="tpu_custom_call" | custom-call | flops 12884901888 | bytes 62914560 | tf_op jit(solution)/shard_map/combine_rows/pallas_call | solution.py:174
  998.8 2.7 convert_element_type.104
  1001.5 2.7 convert_element_type.105
  1004.2 3.7 all-to-all-start.8
  1007.9 34.0 %combine_rows.3 = bf16[6,1024,1024]{2,1,0:T(8,128)(2,1)} custom-call(s32[6,1024,1]{2,1,0:T(8,128)} %copy.181.first_ref, s32[6,1024,1]{2,1,0:T(8,128)} %copy.182.second_ref, bf16[8,2,6,64,1024]{4,3,2,1,0:T(8,128)(2,1)} %all-to-all-done.7.slots_ref, f32[6,1024,1024]{2,1,0:T(8,128)} %combine_rows.2.acc_ref), custom_call_target="tpu_custom_call" | custom-call | flops 12884901888 | bytes 62914560 | tf_op jit(solution)/shard_map/combine_rows/pallas_call | solution.py:174
  1042.0 0.6 fusion.102
  1042.6 0.6 slice.63
  1043.2 42.1 %all_gather.11 = f32[256,128]{1,0:T(8,128)S(1)} all-gather(f32[8,128]{1,0:T(8,128)S(1)} %slice.65), channel_id=1, replica_groups=mesh['ep'=32] {'ep'}, dimensions={0}, use_global_device_ids=true | all-gather | bytes 135168 | tf_op jit(solution)/shard_map/all_gather | solution.py:291
  1085.4 0.8 copy.183
  (86 shorter events, 1.4 us)
Async XLA Ops:
  7.2 4.0 copy-start.6
  7.2 7.2 copy-start.15
  7.2 7.2 copy-start.13
  13.1 84.1 %copy-start.23 = (s32[6,1024]{1,0:T(8,128)}, s32[6,1024]{1,0:T(8,128)S(1)}, u32[]{:S(2)}) copy-start(s32[6,1024]{1,0:T(8,128)S(1)} %get-tuple-element.110) | copy-start | bytes 73732
  19.1 81.5 %copy-start.21 = (s32[6,1024]{1,0:T(8,128)}, s32[6,1024]{1,0:T(8,128)S(1)}, u32[]{:S(2)}) copy-start(s32[6,1024]{1,0:T(8,128)S(1)} %get-tuple-element.97) | copy-start | bytes 73732
  41.7 5.5 copy-start.8
  41.7 145.2 %all-to-all-start = ((bf16[8,2,6,64,1024]{4,3,2,1,0:T(8,128)(2,1)}), bf16[8,2,6,64,1024]{4,3,2,1,0:T(8,128)(2,1)}, u32[]{:S(2)}, u32[]{:S(2)}) async-start(bf16[8,2,6,64,1024]{4,3,2,1,0:T(8,128)(2,1)} %dispatch_rows.4), calls=%async_computation | async-start | bytes 25165824 | tf_op jit(solution)/shard_map/all_to_all | solution.py:197
  97.2 7.0 copy-start.16
  97.2 7.0 copy-start.18
  204.7 5.6 copy-start.4
  204.7 6.2 copy-start.20
  204.7 144.5 %all-to-all-start.2 = ((bf16[8,2,6,64,1024]{4,3,2,1,0:T(8,128)(2,1)}), bf16[8,2,6,64,1024]{4,3,2,1,0:T(8,128)(2,1)}, u32[]{:S(2)}, u32[]{:S(2)}) async-start(bf16[8,2,6,64,1024]{4,3,2,1,0:T(8,128)(2,1)} %dispatch_rows.5), calls=%async_computation.2 | async-start | bytes 25165824 | tf_op jit(solution)/shard_map/all_to_all | solution.py:197
  349.3 144.4 %all-to-all-start.3 = ((bf16[8,2,6,64,1024]{4,3,2,1,0:T(8,128)(2,1)}), bf16[8,2,6,64,1024]{4,3,2,1,0:T(8,128)(2,1)}, u32[]{:S(2)}, u32[]{:S(2)}) async-start(bf16[8,2,6,64,1024]{4,3,2,1,0:T(8,128)(2,1)} %dispatch_rows.6), calls=%async_computation.3 | async-start | bytes 25165824 | tf_op jit(solution)/shard_map/all_to_all | solution.py:197
  354.7 149.7 %all-gather.3.cloned.1.call-start = ((), (), s32[]{:S(2)}) async-start(), calls=%async_computation.11 | async-start | bytes 5242880 | tf_op jit(solution)/shard_map/all_gather | solution.py:207
  493.6 150.6 %all-to-all-start.4 = ((bf16[8,2,6,64,1024]{4,3,2,1,0:T(8,128)(2,1)}), bf16[8,2,6,64,1024]{4,3,2,1,0:T(8,128)(2,1)}, u32[]{:S(2)}, u32[]{:S(2)}) async-start(bf16[8,2,6,64,1024]{4,3,2,1,0:T(8,128)(2,1)} %dispatch_rows.7), calls=%async_computation.4 | async-start | bytes 25165824 | tf_op jit(solution)/shard_map/all_to_all | solution.py:197
  499.0 82.2 %all-gather.5.cloned.1.call-start = ((), (), s32[]{:S(2)}) async-start(), calls=%async_computation.12 | async-start | bytes 5242880 | tf_op jit(solution)/shard_map/all_gather | solution.py:208
  499.7 499.1 %reduce-scatter.3.cloned.1.call-start = ((), (), s32[]{:S(2)}) async-start(), calls=%async_computation.13 | async-start | bytes 10485760 | tf_op jit(solution)/shard_map/reduce_scatter | solution.py:259
  499.8 0.6 copy-start.2
  707.3 144.3 %all-to-all-start.5 = ((bf16[8,2,6,64,1024]{4,3,2,1,0:T(8,128)(2,1)}), bf16[8,2,6,64,1024]{4,3,2,1,0:T(8,128)(2,1)}, u32[]{:S(2)}, u32[]{:S(2)}) async-start(bf16[8,2,6,64,1024]{4,3,2,1,0:T(8,128)(2,1)} %get-tuple-element.58), calls=%async_computation.5 | async-start | bytes 25165824 | tf_op jit(solution)/shard_map/all_to_all | solution.py:197
  712.7 288.8 %reduce-scatter.5.cloned.1.call-start = ((), (), s32[]{:S(2)}) async-start(), calls=%async_computation.14 | async-start | bytes 10485760 | tf_op jit(solution)/shard_map/reduce_scatter | solution.py:260
  712.7 1.9 copy-start.1
  716.4 2.4 copy-start.9
  858.8 5.7 copy-start.10
  858.8 145.4 %all-to-all-start.7 = ((bf16[8,2,6,64,1024]{4,3,2,1,0:T(8,128)(2,1)}), bf16[8,2,6,64,1024]{4,3,2,1,0:T(8,128)(2,1)}, u32[]{:S(2)}, u32[]{:S(2)}) async-start(bf16[8,2,6,64,1024]{4,3,2,1,0:T(8,128)(2,1)} %get-tuple-element.61), calls=%async_computation.7 | async-start | bytes 25165824 | tf_op jit(solution)/shard_map/all_to_all | solution.py:197
  864.5 2.3 copy-start.11
  864.6 4.5 copy-start.5
  866.8 4.4 copy-start.12
  873.5 12.5 %copy-start.3 = (f32[8,4,384]{2,1,0:T(4,128)S(1)}, f32[8,4,384]{2,1,0:T(4,128)}, u32[]{:S(2)}) copy-start(f32[8,4,384]{2,1,0:T(4,128)} %copy-done.2) | copy-start | bytes 147460
  873.5 14.4 %copy-start.25 = (f32[32]{0:T(128)S(1)}, f32[32]{0:T(128)}, u32[]{:S(2)}) copy-start(f32[32]{0:T(128)} %get-tuple-element.90) | copy-start | bytes 388
  873.5 14.6 %copy-start.14 = (s32[6,1024]{1,0:T(8,128)S(1)}, s32[6,1024]{1,0:T(8,128)}, u32[]{:S(2)}) copy-start(s32[6,1024]{1,0:T(8,128)} %param.18) | copy-start | bytes 73732
  873.5 14.6 %copy-start.22 = (s32[6,1024]{1,0:T(8,128)S(1)}, s32[6,1024]{1,0:T(8,128)}, u32[]{:S(2)}) copy-start(s32[6,1024]{1,0:T(8,128)} %copy-done.21) | copy-start | bytes 73732
  873.5 16.6 %copy-start.7 = (s32[6,1024]{1,0:T(8,128)S(1)}, s32[6,1024]{1,0:T(8,128)}, u32[]{:S(2)}) copy-start(s32[6,1024]{1,0:T(8,128)} %param.17) | copy-start | bytes 73732
  873.5 16.6 %copy-start.24 = (s32[6,1024]{1,0:T(8,128)S(1)}, s32[6,1024]{1,0:T(8,128)}, u32[]{:S(2)}) copy-start(s32[6,1024]{1,0:T(8,128)} %copy-done.23) | copy-start | bytes 73732
  885.9 6.2 copy-start.17
  885.9 6.2 copy-start.19
  954.3 7.5 copy-start
  1004.2 37.7 %all-to-all-start.8 = ((f32[32,16,128]{2,1,0:T(8,128)}), f32[32,16,128]{2,1,0:T(8,128)S(1)}, u32[]{:S(2)}, u32[]{:S(2)}) async-start(f32[32,16,128]{2,1,0:T(8,128)} %pad_maximum_fusion), calls=%async_computation.8 | async-start | bytes 524288 | tf_op jit(solution)/shard_map/all_to_all | solution.py:289
Sparse Core Ops, SparseCore 0:
  357.0 79.8 all-gather.2
  501.4 79.7 all-gather.4
  707.5 143.1 reduce-scatter.2
  852.9 145.2 reduce-scatter.4
where the time goes:
time: 1100 us
  waiting for transfers between devices  506 us (46%)
  Pallas kernels  281 us (26%)
  other arithmetic  125 us (11%)
  blocking collectives  67.1 us (6%)
  starting transfers between devices  36.8 us (3%)
  matrix products  35.7 us (3%)
  local copies, waits for them, and re-layouts  25.8 us (2%)
  between operations  17.9 us (2%)
    all_to_all x6, waiting for transfers between devices, swap(): lax.all_to_all(value, 'ep', 0, 0, axis_index_groups=plane_groups, tiled=T...  427 us
    pallas_call x2, Pallas kernels, expert_part(): pl.pallas_call(expert_kernel, grid=(parts, peers), in_specs=[block, block...  126 us
    pallas_call x4, Pallas kernels, dispatch(): pl.pallas_call(dispatch_kernel, grid=(groups,), in_specs=[pl.BlockSpec((1...  85.3 us
    all_gather x1, waiting for transfers between devices, layer(): lax.all_gather(w_out_loc, 'ep', axis=0, axis_index_groups=line_groups, ti...  76.8 us
    pallas_call x2, Pallas kernels, combine(): pl.pallas_call(kernel, grid=(groups, seq_len // tile), in_specs=[column,...  69.8 us
    sub x1, other arithmetic, layer(): grad_prob - jnp.sum(router_prob * grad_prob, axis=-1, keepdims=True)  62.2 us
    all_gather x1, blocking collectives, layer(): lax.all_gather(total[:rows], 'ep', axis=0, tiled=True)  42.1 us
    div x1, other arithmetic, layer(): router_prob = jax.nn.softmax(logits, axis=-1)  38.7 us
  transfers between devices with their start and end apart: 11, of which 5 were waited for; matrix products, arithmetic and copies ran while one was open for 15% of the time, Pallas kernels for 18%

commit v1 on v0

--- a/solution.py
+++ b/solution.py
@@ -11,7 +11,7 @@
 BF16 = jnp.bfloat16
 I32 = jnp.int32
 PLANE = 8
-CHUNKS = 2
+LAST = 1
 VMEM_LIMIT = 60 * 1024 * 1024
 
 
@@ -38,13 +38,15 @@
     per_peer = parts * cap_rows
     rows = rows_ref[0]
 
-    @pl.loop(0, peers, step=2)
+    step = 4 if parts == 1 else 2
+
+    @pl.loop(0, peers, step=step)
     def _(peer):
-        slot = lax.broadcasted_iota(I32, (2 * per_peer, rows.shape[0]), 0) + peer * per_peer
+        slot = lax.broadcasted_iota(I32, (step * per_peer, rows.shape[0]), 0) + peer * per_peer
         hit = (slot == first_ref[0]) | (slot == second_ref[0])
         table = jnp.where(hit, 1.0, 0.0).astype(BF16)
         picked = jnp.dot(table, rows, preferred_element_type=F32).astype(BF16)
-        out_ref[pl.ds(peer, 2)] = picked.reshape(2, parts, 1, cap_rows, hidden)
+        out_ref[pl.ds(peer, step)] = picked.reshape(step, parts, 1, cap_rows, hidden)
 
 
 def dispatch(first_slot, second_slot, rows, parts, cap_rows):
@@ -114,15 +116,15 @@
         d_in_ref[0] += d_in
 
 
-def expert_part(part, parts, x_slots, r_slots, norms, w_in, w_out, earlier):
+def expert_part(start, parts, x_slots, r_slots, norms, w_in, w_out, earlier):
     peers, _, groups, cap_rows, hidden = x_slots.shape
     _, _, ff_dim = w_in.shape
     rows = groups * cap_rows
     block = pl.BlockSpec((1, 1, groups, cap_rows, hidden), lambda e, s: (s, e, 0, 0, 0))
     column = pl.BlockSpec((1, 1, rows, 1), lambda e, s: (s, e, 0, 0))
-    norm_column = pl.BlockSpec((1, 1, rows, 1), lambda e, s: (s, parts * part + e, 0, 0))
-    in_block = pl.BlockSpec((1, hidden, ff_dim), lambda e, s: (parts * part + e, 0, 0))
-    out_block = pl.BlockSpec((1, ff_dim, hidden), lambda e, s: (parts * part + e, 0, 0))
+    norm_column = pl.BlockSpec((1, 1, rows, 1), lambda e, s: (s, start + e, 0, 0))
+    in_block = pl.BlockSpec((1, hidden, ff_dim), lambda e, s: (start + e, 0, 0))
+    out_block = pl.BlockSpec((1, ff_dim, hidden), lambda e, s: (start + e, 0, 0))
     return pl.pallas_call(
         expert_kernel,
         grid=(parts, peers),
@@ -149,13 +151,13 @@
     return acc + dot_nn(jnp.where(hit, 1.0, 0.0).astype(BF16), slots)
 
 
-def combine_start_kernel(first_ref, second_ref, slots_ref, r_ref, logit_ref, gate_ref, out_ref):
-    acc = r_ref[0].astype(F32) + dot_nn(logit_ref[0], gate_ref[...])
-    out_ref[0] = gathered(first_ref, second_ref, slots_ref, acc)
-
-
-def combine_more_kernel(first_ref, second_ref, slots_ref, acc_ref, out_ref):
-    out_ref[0] = gathered(first_ref, second_ref, slots_ref, acc_ref[0]).astype(out_ref.dtype)
+def combine_start_kernel(first_ref, second_ref, slots_ref, r_ref, out_ref):
+    out_ref[0] = gathered(first_ref, second_ref, slots_ref, r_ref[0].astype(F32))
+
+
+def combine_more_kernel(first_ref, second_ref, slots_ref, acc_ref, logit_ref, gate_ref, out_ref):
+    acc = acc_ref[0] + dot_tn(logit_ref[0], gate_ref[...])
+    out_ref[0] = gathered(first_ref, second_ref, slots_ref, acc).astype(out_ref.dtype)
 
 
 def combine(first_slot, second_slot, slots, extra, out_type):
@@ -166,11 +168,11 @@
     wide = pl.BlockSpec((1, tile, hidden), lambda g, t: (g, t, 0))
     block = pl.BlockSpec((peers, parts, 1, cap_rows, hidden), lambda g, t: (0, 0, g, 0, 0))
     if len(extra) == 1:
-        kernel, extra_specs = combine_more_kernel, [wide]
+        kernel, extra_specs = combine_start_kernel, [wide]
     else:
-        experts = extra[1].shape[-1]
-        kernel = combine_start_kernel
-        extra_specs = [wide, pl.BlockSpec((1, tile, experts), lambda g, t: (g, t, 0)), pl.BlockSpec((experts, hidden), lambda g, t: (0, 0))]
+        experts = extra[1].shape[1]
+        kernel = combine_more_kernel
+        extra_specs = [wide, pl.BlockSpec((1, experts, tile), lambda g, t: (g, 0, t)), pl.BlockSpec((experts, hidden), lambda g, t: (0, 0))]
     return pl.pallas_call(
         kernel,
         grid=(groups, seq_len // tile),
@@ -180,7 +182,7 @@
         compiler_params=pltpu.CompilerParams(vmem_limit_bytes=VMEM_LIMIT),
         cost_estimate=pl.CostEstimate(flops=2 * groups * seq_len * peers * parts * cap_rows * hidden, bytes_accessed=10 * groups * seq_len * hidden, transcendentals=0),
         name='combine_rows',
-    )(first_slot[..., None], second_slot[..., None], slots, *extra)
+    )(first_slot, second_slot, slots, *extra)
 
 
 def after(value, *others):
@@ -202,7 +204,8 @@
         cap_rows = 2 * seq_len // experts
         tokens_all = local_groups * ep_size * seq_len
         numel = tokens_all * hidden
-        parts = planes // CHUNKS
+        starts = (0, planes - LAST)
+        parts = (planes - LAST, LAST)
 
         w_in = lax.all_gather(w_in_loc, 'ep', axis=0, axis_index_groups=line_groups, tiled=True)
         w_out = lax.all_gather(w_out_loc, 'ep', axis=0, axis_index_groups=line_groups, tiled=True)
@@ -210,14 +213,15 @@
         first_hot, second_hot, first_count, pos_first, pos_second = route_slots(first_ids, second_ids, keep_ids, experts, cap_rows)
 
         def part_slot(ids, pos, part):
-            z, peer = ids // PLANE, ids % PLANE
-            here = (pos >= 0) & (z // parts == part)
-            return jnp.where(here, (peer * parts + z % parts) * cap_rows + pos, -1)
-
-        slots = [(part_slot(first_ids, pos_first, c), part_slot(second_ids, pos_second, c)) for c in range(CHUNKS)]
+            z, peer = ids // PLANE - starts[part], ids % PLANE
+            here = (pos >= 0) & (z >= 0) & (z < parts[part])
+            return jnp.where(here, (peer * parts[part] + z) * cap_rows + pos, -1)
+
+        slots = [(part_slot(first_ids, pos_first, c), part_slot(second_ids, pos_second, c)) for c in range(2)]
+        columns = [(a[..., None], b[..., None]) for a, b in slots]
 
         def send(rows, part):
-            return dispatch(*slots[part], rows, parts, cap_rows)
+            return dispatch(*slots[part], rows, parts[part], cap_rows)
 
         sent_x = [send(x_loc, 0)]
         x_late = after(x_loc, sent_x[0])
@@ -238,33 +242,38 @@
         sent_r = [send(r_loc, 0)]
         got_x = [swap(sent_x[0])]
         counts = jnp.sum(first_count, axis=0)
-        counts = jnp.zeros((PLANE, 1, local_groups * cap_rows), F32).at[:, :, :experts].set(counts)
-        note = jnp.tile(jnp.concatenate([norm_slots.astype(F32), counts], axis=1), (planes, 1, 1))
+        high = jnp.floor(counts / 64)
+        digits = jnp.zeros((PLANE, 4, 128), BF16).at[:, 0, :experts].set(high.astype(BF16)).at[:, 1, :experts].set((counts - 64 * high).astype(BF16))
+        norm_rows = planes * local_groups * cap_rows // 128
+        note = jnp.tile(jnp.concatenate([norm_slots.reshape(PLANE, norm_rows, 128), digits], axis=1), (planes, 1, 1))
         note = lax.all_to_all(after(note, got_x[0], sent_r[0]), 'ep', 0, 0, tiled=True)
-        frac_first = jnp.sum(note[:, planes, :experts], axis=0) / tokens_all
+        digits = jnp.sum(note[:, norm_rows:norm_rows + 2, :experts].astype(F32), axis=0)
+        frac_first = (64 * digits[0] + digits[1]) / tokens_all
         got_r = [swap(after(sent_r[0], note))]
-        norms = lax.dynamic_slice_in_dim(note, lax.axis_index('ep') // PLANE * PLANE, PLANE, 0)[:, :planes, :, None]
-        for c in range(1, CHUNKS):
-            sent_x.append(send(x_late, c))
-            got_x.append(swap(after(sent_x[c], got_r[c - 1])))
-            sent_r.append(send(after(r_loc, sent_r[c - 1]), c))
-            got_r.append(swap(after(sent_r[c], got_x[c])))
+        norms = lax.dynamic_slice_in_dim(note, lax.axis_index('ep') // PLANE * PLANE, PLANE, 0)[:, :norm_rows]
+        norms = norms.astype(F32).reshape(PLANE, planes, local_groups * cap_rows, 1)
+        plain_sum = jnp.einsum('gsh,gsh->', x_late, r_loc, preferred_element_type=F32)
+        sent_x.append(send(x_late, 1))
+        got_x.append(swap(after(sent_x[1], got_r[0])))
+        sent_r.append(send(after(r_loc, sent_r[0]), 1))
+        got_r.append(swap(after(sent_r[1], got_x[1])))
+        norms, plain_sum, columns = lax.optimization_barrier((norms, plain_sum, columns))
         grads = ()
         grad_slots = []
         dots = []
-        for c in range(CHUNKS):
-            out_slots, out_dots, *grads = expert_part(c, parts, got_x[c], got_r[c], norms, w_in, w_out, grads)
+        for c in range(2):
+            out_slots, out_dots, *grads = expert_part(starts[c], parts[c], got_x[c], got_r[c], norms, w_in, w_out, grads)
             grad_slots.append(out_slots)
             dots.append(out_dots)
-        grad_w_in = lax.psum_scatter(grads[0], 'ep', scatter_dimension=0, axis_index_groups=line_groups, tiled=True).astype(BF16)
-        grad_w_out = lax.psum_scatter(grads[1], 'ep', scatter_dimension=0, axis_index_groups=line_groups, tiled=True).astype(BF16)
+        d_in = lax.psum_scatter(grads[0], 'ep', scatter_dimension=0, axis_index_groups=line_groups, tiled=True)
+        d_out = lax.psum_scatter(grads[1], 'ep', scatter_dimension=0, axis_index_groups=line_groups, tiled=True)
+        grad_w_in, grad_w_out = d_in.astype(BF16), d_out.astype(BF16)
         dots = jnp.concatenate([d[..., 0] for d in dots], axis=1)
         moe_sum = jnp.sum(dots * norms[..., 0])
 
         back = [swap(after(grad_slots[0], got_r[-1]))]
         dots_back = swap(after(dots.astype(BF16), back[0]))
-        for c in range(1, CHUNKS):
-            back.append(swap(after(grad_slots[c], dots_back if c == 1 else back[c - 1])))
+        back.append(swap(after(grad_slots[1], dots_back)))
         dots_back = dots_back.reshape(PLANE, planes, local_groups, cap_rows).transpose(2, 1, 0, 3).reshape(local_groups, experts, cap_rows)
 
         grad_norm_first = jnp.sum(jnp.einsum('gse,gec->gsc', first_hot, dots_back, preferred_element_type=F32) * place_first, axis=-1)
@@ -275,12 +284,11 @@
         grad_prob = grad_gate_first[..., None] * first_hot + grad_gate_second[..., None] * second_hot + (ALPHA * hidden * experts) * frac_first
         grad_logits = router_prob * (grad_prob - jnp.sum(router_prob * grad_prob, axis=-1, keepdims=True))
         grad_logits_bf = lax.optimization_barrier(grad_logits.astype(BF16))
-        grad_x = combine(*slots[0], back[0], (r_loc, grad_logits_bf, w_gate.T), F32 if CHUNKS > 1 else BF16)
-        for c in range(1, CHUNKS):
-            grad_x = combine(*slots[c], back[c], (grad_x,), BF16 if c == CHUNKS - 1 else F32)
+        grad_x = combine(*columns[0], back[0], (r_loc,), F32)
+        grad_x = combine(*columns[1], back[1], (grad_x, jnp.swapaxes(grad_logits_bf, 1, 2), w_gate.T), BF16)
         grad_gate_w = jnp.einsum('gsh,gse->he', x_loc, grad_logits_bf, preferred_element_type=F32)
 
-        dot_sum = jnp.einsum('gsh,gsh->', x_late, r_loc, preferred_element_type=F32) + moe_sum
+        dot_sum = plain_sum + moe_sum
         local_stats = jnp.concatenate([jnp.sum(router_prob, axis=(0, 1)), dot_sum[None]])
         rows = hidden * experts // ep_size // 128
         own = grad_gate_w.reshape(ep_size, rows, 128)
@@ -288,7 +296,7 @@
         packed = jnp.concatenate([own, jnp.broadcast_to(shared, (ep_size, 8, 128))], axis=1)
         packed = lax.all_to_all(after(packed, back[-1]), 'ep', 0, 0, tiled=True)
         total = jnp.sum(packed, axis=0)
-        grad_gate_w = lax.all_gather(total[:rows], 'ep', axis=0, tiled=True).reshape(hidden, experts)
+        grad_gate_w = lax.all_to_all(jnp.broadcast_to(total[:rows], (ep_size, rows, 128)), 'ep', 0, 0, tiled=True).reshape(hidden, experts)
         global_stats = total[rows]
         mean_prob = global_stats[:experts] / tokens_all
         loss_value = global_stats[experts] / numel + ALPHA * experts * jnp.sum(frac_first * mean_prob)

time: 1100 us -> 1090 us (level)
  waiting for transfers between devices: 506 us -> 658 us
  other arithmetic: 125 us -> 23.5 us
  blocking collectives: 67.1 us -> 19.9 us
  matrix products: 35.7 us -> 22.1 us
    all_to_all x6, waiting for transfers between devices: 427 us -> 656 us  [swap(): lax.all_to_all(value, 'ep', 0, 0, axis_index_groups=plane_groups, tiled=T...]
    all_gather x1, waiting for transfers between devices: 76.8 us -> 0.01 us  [layer(): lax.all_gather(w_out_loc, 'ep', axis=0, axis_index_groups=line_groups, ti...]
    sub x1, other arithmetic: 62.2 us -> 0.42 us  [layer(): grad_prob - jnp.sum(router_prob * grad_prob, axis=-1, keepdims=True)]
    all_gather x1 -> x0, blocking collectives: 42.1 us -> none  [layer(): lax.all_gather(total[:rows], 'ep', axis=0, tiled=True)]
    div x1 -> x0, other arithmetic: 38.7 us -> none  [layer(): router_prob = jax.nn.softmax(logits, axis=-1)]
    optimization_barrier x0 -> x5, local copies, waits for them, and re-layouts: none -> 12.8 us  [layer(): lax.optimization_barrier((norms, plain_sum, columns))]
    broadcast_in_dim x5 -> x1, local copies, waits for them, and re-layouts: 12.8 us -> 0.66 us  [layer(): jnp.broadcast_to(total[:rows], (ep_size, rows, 128))]
  transfers between devices with their start and end apart: 11 -> 12, of which waited for: 5 -> 5; matrix products, arithmetic and copies ran while one was open for 15% -> 5% of each run, Pallas kernels for 18% -> 20%
where the time goes in v1:
time: 1090 us; the launch traced here: 1080 us
  waiting for transfers between devices  658 us (60%)
  Pallas kernels  280 us (26%)
  starting transfers between devices  41.1 us (4%)
  other arithmetic  23.5 us (2%)
  local copies, waits for them, and re-layouts  22.5 us (2%)
  matrix products  22.1 us (2%)
  blocking collectives  19.9 us (2%)
  between operations  18 us (2%)
    all_to_all x6, waiting for transfers between devices, swap(): lax.all_to_all(value, 'ep', 0, 0, axis_index_groups=plane_groups, tiled=T...  656 us
    pallas_call x2, Pallas kernels, expert_part(): pl.pallas_call(expert_kernel, grid=(parts, peers), in_specs=[block, block...  126 us
    pallas_call x4, Pallas kernels, dispatch(): pl.pallas_call(dispatch_kernel, grid=(groups,), in_specs=[pl.BlockSpec((1...  82.9 us
    pallas_call x2, Pallas kernels, combine(): pl.pallas_call(kernel, grid=(groups, seq_len // tile), in_specs=[column,...  70.8 us
    all_to_all x6, starting transfers between devices, swap(): lax.all_to_all(value, 'ep', 0, 0, axis_index_groups=plane_groups, tiled=T...  32.5 us
  transfers between devices with their start and end apart: 12, of which 5 were waited for; matrix products, arithmetic and copies ran while one was open for 5% of the time, Pallas kernels for 20%

profile of v1, /device:TPU:0, one launch (start us, length us, event | category | flops | bytes accessed | tf_op | source)
XLA Modules:
  0.0 1084.9 jit_solution(18337511831705748003)
XLA Ops:
  7.2 1.6 fusion.36
  8.8 0.9 convert_reduce_fusion.1
  9.7 0.8 add_select_fusion.5
  10.5 0.6 copy.102.first_ref
  11.2 0.8 convert_element_type.93
  11.9 1.6 fusion.33
  13.7 0.6 copy.103.second_ref
  14.3 28.2 %dispatch_rows.4 = bf16[8,3,6,64,1024]{4,3,2,1,0:T(8,128)(2,1)} custom-call(s32[6,1,1024]{2,1,0:T(1,128)} %copy.102.first_ref, s32[6,1,1024]{2,1,0:T(1,128)} %copy.103.second_ref, bf16[6,1024,1024]{2,1,0:T(8,128)(2,1)} %rows_ref.4), custom_call_target="tpu_custom_call" | custom-call | flops 19327352832 | bytes 25165824 | tf_op jit(solution)/shard_map/dispatch_rows/pallas_call | solution.py:55
  42.5 6.0 all-to-all-start
  48.6 10.1 fusion.95
  58.7 0.4 fusion.10
  59.1 0.2 copy-done.8
  59.3 0.4 fusion.41
  59.9 0.3 scatter.19
  60.2 28.3 %dispatch_rows.5 = bf16[8,3,6,64,1024]{4,3,2,1,0:T(8,128)(2,1)} custom-call(s32[6,1,1024]{2,1,0:T(1,128)} %copy.102.first_ref, s32[6,1,1024]{2,1,0:T(1,128)} %copy.103.second_ref, bf16[6,1024,1024]{2,1,0:T(8,128)(2,1)} %r_ref.1), custom_call_target="tpu_custom_call" | custom-call | flops 19327352832 | bytes 25165824 | tf_op jit(solution)/shard_map/dispatch_rows/pallas_call | solution.py:55
  88.5 167.2 %all-to-all-done.x_ref = bf16[8,3,6,64,1024]{4,3,2,1,0:T(8,128)(2,1)} async-done(((bf16[8,3,6,64,1024]{4,3,2,1,0:T(8,128)(2,1)}), bf16[8,3,6,64,1024]{4,3,2,1,0:T(8,128)(2,1)}, u32[]{:S(2)}, u32[]{:S(2)}) %all-to-all-start) | async-done | bytes 18874400 | tf_op jit(solution)/shard_map/all_to_all | solution.py:199
  255.7 12.8 %all_to_all.50 = bf16[32,16,128]{2,1,0:T(8,128)(2,1)S(1)} all-to-all(bf16[32,16,128]{2,1,0:T(8,128)(2,1)S(1)} %bitcast.88), channel_id=1, replica_groups=mesh['ep'=32] {'ep'}, dimensions={0} | all-to-all | bytes 262144 | tf_op jit(solution)/shard_map/all_to_all | solution.py:249
  268.5 5.9 all-to-all-start.2
  274.4 0.7 all-gather.3.cloned.1.call-update
  275.2 0.7 all-gather.5.cloned.1.call-update
  275.9 0.6 copy.109.first_ref
  276.5 0.6 broadcast_in_dim.39.second_ref
  277.1 13.3 %dispatch_rows.6 = bf16[8,1,6,64,1024]{4,3,2,1,0:T(8,128)(2,1)} custom-call(s32[6,1,1024]{2,1,0:T(1,128)} %copy.109.first_ref, s32[6,1,1024]{2,1,0:T(1,128)} %broadcast_in_dim.39.second_ref, bf16[6,1024,1024]{2,1,0:T(8,128)(2,1)} %rows_ref.4), custom_call_target="tpu_custom_call" | custom-call | flops 6442450944 | bytes 25165824 | tf_op jit(solution)/shard_map/dispatch_rows/pallas_call | solution.py:55
  290.4 190.4 %all-to-all-done.2.r_ref = bf16[8,3,6,64,1024]{4,3,2,1,0:T(8,128)(2,1)} async-done(((bf16[8,3,6,64,1024]{4,3,2,1,0:T(8,128)(2,1)}), bf16[8,3,6,64,1024]{4,3,2,1,0:T(8,128)(2,1)}, u32[]{:S(2)}, u32[]{:S(2)}) %all-to-all-start.2) | async-done | bytes 18874400 | tf_op jit(solution)/shard_map/all_to_all | solution.py:199
  480.8 4.8 all-to-all-start.3
  485.6 13.1 %dispatch_rows.7 = bf16[8,1,6,64,1024]{4,3,2,1,0:T(8,128)(2,1)} custom-call(s32[6,1,1024]{2,1,0:T(1,128)} %copy.109.first_ref, s32[6,1,1024]{2,1,0:T(1,128)} %broadcast_in_dim.39.second_ref, bf16[6,1024,1024]{2,1,0:T(8,128)(2,1)} %r_ref.1), custom_call_target="tpu_custom_call" | custom-call | flops 6442450944 | bytes 25165824 | tf_op jit(solution)/shard_map/dispatch_rows/pallas_call | solution.py:55
  498.7 12.2 %fusion.3 = f32[]{:T(128)} fusion(bf16[6,1024,1024]{2,1,0:T(8,128)(2,1)} %r_ref.1, bf16[6,1024,1024]{2,1,0:T(8,128)(2,1)} %rows_ref.4), kind=kLoop, calls=%fused_computation.4 | loop fusion | flops 25165824 | bytes 25165828 | tf_op jit(solution)/shard_map/gsh,gsh->/dot_general | solution.py:255
  511.0 46.2 %all-to-all-done.3.x_ref = bf16[8,1,6,64,1024]{4,3,2,1,0:T(8,128)(2,1)} async-done(((bf16[8,1,6,64,1024]{4,3,2,1,0:T(8,128)(2,1)}), bf16[8,1,6,64,1024]{4,3,2,1,0:T(8,128)(2,1)}, u32[]{:S(2)}, u32[]{:S(2)}) %all-to-all-start.3) | async-done | bytes 6291488 | tf_op jit(solution)/shard_map/all_to_all | solution.py:199
  557.1 4.9 all-to-all-start.4
  562.2 4.0 copy.107.norm_ref
  566.2 92.4 %expert_part.2 = (bf16[8,3,6,64,1024]{4,3,2,1,0:T(8,128)(2,1)}, f32[8,3,384,1]{3,2,1,0:T(8,128)}, f32[4,1024,512]{2,1,0:T(8,128)}, f32[4,512,1024]{2,1,0:T(8,128)}) custom-call(bf16[8,3,6,64,1024]{4,3,2,1,0:T(8,128)(2,1)} %all-to-all-done.x_ref, bf16[8,3,6,64,1024]{4,3,2,1,0:T(8,128)(2,1)} %all-to-all-done.2.r_ref, f32[8,4,384,1]{3,2,1,0:T(8,128)} %copy.107.norm_ref, ...), custom_call_target="tpu_custom_call" | custom-call | flops 57982058496 | bytes 56623104 | tf_op jit(solution)/shard_map/expert_part/pallas_call | solution.py:128
  658.6 33.7 %expert_part.3 = (bf16[8,1,6,64,1024]{4,3,2,1,0:T(8,128)(2,1)}, f32[8,1,384,1]{3,2,1,0:T(8,128)}, f32[4,1024,512]{2,1,0:T(8,128)}, f32[4,512,1024]{2,1,0:T(8,128)}) custom-call(bf16[8,1,6,64,1024]{4,3,2,1,0:T(8,128)(2,1)} %all-to-all-done.3.x_ref, bf16[8,1,6,64,1024]{4,3,2,1,0:T(8,128)(2,1)} %all-to-all-done.4.r_ref, ...), custom_call_target="tpu_custom_call", output_to_operand_aliasing={{2}: (5, {}), {3}: (6, {})} | custom-call | flops 19327352832 | bytes 18874368 | tf_op jit(solution)/shard_map/expert_part/pallas_call | solution.py:128
  692.4 6.0 all-to-all-start.5
  698.4 0.5 reduce-scatter.5.cloned.1.call-update
  698.9 3.8 copy.108
  702.7 0.5 reduce.9
  703.2 201.5 %all-to-all-done.5.slots_ref = bf16[8,3,6,64,1024]{4,3,2,1,0:T(8,128)(2,1)} async-done(((bf16[8,3,6,64,1024]{4,3,2,1,0:T(8,128)(2,1)}), bf16[8,3,6,64,1024]{4,3,2,1,0:T(8,128)(2,1)}, u32[]{:S(2)}, u32[]{:S(2)}) %all-to-all-start.5) | async-done | bytes 18874400 | tf_op jit(solution)/shard_map/all_to_all | solution.py:199
  904.8 7.2 all_to_all.51
  911.9 5.0 all-to-all-start.7
  916.9 2.2 copy.119.first_ref
  919.1 2.2 copy.120.second_ref
  921.4 2.2 copy.117.first_ref
  923.5 2.2 copy.118.second_ref
  925.8 0.7 fusion.78
  927.8 0.1 reshape.224
  927.9 0.5 multiply_reduce_fusion.1
  928.5 0.5 multiply_reduce_fusion
  929.0 0.4 fusion.32
  929.5 7.1 convolution_bitcast_fusion
  936.5 0.2 copy.115
  936.8 0.2 reshape.226
  937.0 0.8 pad_maximum_fusion
  937.7 50.5 %all-to-all-done.7.slots_ref = bf16[8,1,6,64,1024]{4,3,2,1,0:T(8,128)(2,1)} async-done(((bf16[8,1,6,64,1024]{4,3,2,1,0:T(8,128)(2,1)}), bf16[8,1,6,64,1024]{4,3,2,1,0:T(8,128)(2,1)}, u32[]{:S(2)}, u32[]{:S(2)}) %all-to-all-start.7) | async-done | bytes 6291488 | tf_op jit(solution)/shard_map/all_to_all | solution.py:199
  988.2 2.6 all-to-all-start.8
  990.8 40.3 %combine_rows.2.acc_ref = f32[6,1024,1024]{2,1,0:T(8,128)} custom-call(s32[6,1024,1]{2,1,0:T(8,128)} %copy.117.first_ref, s32[6,1024,1]{2,1,0:T(8,128)} %copy.118.second_ref, bf16[8,3,6,64,1024]{4,3,2,1,0:T(8,128)(2,1)} %all-to-all-done.5.slots_ref, bf16[6,1024,1024]{2,1,0:T(8,128)(2,1)} %r_ref.1), custom_call_target="tpu_custom_call" | custom-call | flops 19327352832 | bytes 62914560 | tf_op jit(solution)/shard_map/combine_rows/pallas_call | solution.py:176
  1031.1 2.7 convert_element_type.110
  1033.8 2.7 convert_element_type.111
  1036.6 0.7 broadcast_in_dim.81
  1037.3 5.8 all-to-all-start.9
  1043.1 30.5 %combine_rows.3 = bf16[6,1024,1024]{2,1,0:T(8,128)(2,1)} custom-call(s32[6,1024,1]{2,1,0:T(8,128)} %copy.119.first_ref, s32[6,1024,1]{2,1,0:T(8,128)} %copy.120.second_ref, bf16[8,1,6,64,1024]{4,3,2,1,0:T(8,128)(2,1)} %all-to-all-done.7.slots_ref, f32[6,1024,1024]{2,1,0:T(8,128)} %combine_rows.2.acc_ref, bf16[6,32,1024]{2,1,0:T(8,128)(2,1)} %bitcast.87, ...), custom_call_target="tpu_custom_call" | custom-call | flops 6442450944 | bytes 62914560 | tf_op jit(solution)/shard_map/combine_rows/pallas_call | solution.py:176
  1073.6 0.6 slice.99
  1074.9 0.7 fusion.90
  1076.3 0.2 reshape.228
  1076.5 0.8 copy.121
  (68 shorter events, 0.9 us)
Async XLA Ops:
  7.2 6.4 copy-start.5
  7.2 6.4 copy-start.4
  10.5 32.0 %copy-start.2 = (s32[6,1024]{1,0:T(8,128)}, s32[6,1024]{1,0:T(8,128)S(1)}, u32[]{:S(2)}) copy-start(s32[6,1024]{1,0:T(8,128)S(1)} %get-tuple-element.123) | copy-start | bytes 73732
  10.5 48.6 %copy-start.12 = (s32[6,1024]{1,0:T(8,128)}, s32[6,1024]{1,0:T(8,128)S(1)}, u32[]{:S(2)}) copy-start(s32[6,1024]{1,0:T(8,128)S(1)} %get-tuple-element.126) | copy-start | bytes 73732
  42.5 6.1 copy-start.6
  42.5 213.2 %all-to-all-start = ((bf16[8,3,6,64,1024]{4,3,2,1,0:T(8,128)(2,1)}), bf16[8,3,6,64,1024]{4,3,2,1,0:T(8,128)(2,1)}, u32[]{:S(2)}, u32[]{:S(2)}) async-start(bf16[8,3,6,64,1024]{4,3,2,1,0:T(8,128)(2,1)} %dispatch_rows.4), calls=%async_computation | async-start | bytes 37748736 | tf_op jit(solution)/shard_map/all_to_all | solution.py:199
  58.7 0.6 copy-start.8
  58.7 1.0 copy-start.10
  268.5 212.3 %all-to-all-start.2 = ((bf16[8,3,6,64,1024]{4,3,2,1,0:T(8,128)(2,1)}), bf16[8,3,6,64,1024]{4,3,2,1,0:T(8,128)(2,1)}, u32[]{:S(2)}, u32[]{:S(2)}) async-start(bf16[8,3,6,64,1024]{4,3,2,1,0:T(8,128)(2,1)} %dispatch_rows.5), calls=%async_computation.2 | async-start | bytes 37748736 | tf_op jit(solution)/shard_map/all_to_all | solution.py:199
  274.4 291.8 %all-gather.3.cloned.1.call-start = ((), (), s32[]{:S(2)}) async-start(), calls=%async_computation.12 | async-start | bytes 5242880 | tf_op jit(solution)/shard_map/all_gather | solution.py:210
  275.1 291.1 %all-gather.5.cloned.1.call-start = ((), (), s32[]{:S(2)}) async-start(), calls=%async_computation.13 | async-start | bytes 5242880 | tf_op jit(solution)/shard_map/all_gather | solution.py:211
  480.8 76.3 %all-to-all-start.3 = ((bf16[8,1,6,64,1024]{4,3,2,1,0:T(8,128)(2,1)}), bf16[8,1,6,64,1024]{4,3,2,1,0:T(8,128)(2,1)}, u32[]{:S(2)}, u32[]{:S(2)}) async-start(bf16[8,1,6,64,1024]{4,3,2,1,0:T(8,128)(2,1)} %dispatch_rows.6), calls=%async_computation.3 | async-start | bytes 12582912 | tf_op jit(solution)/shard_map/all_to_all | solution.py:199
  557.1 101.5 %all-to-all-start.4 = ((bf16[8,1,6,64,1024]{4,3,2,1,0:T(8,128)(2,1)}), bf16[8,1,6,64,1024]{4,3,2,1,0:T(8,128)(2,1)}, u32[]{:S(2)}, u32[]{:S(2)}) async-start(bf16[8,1,6,64,1024]{4,3,2,1,0:T(8,128)(2,1)} %dispatch_rows.7), calls=%async_computation.4 | async-start | bytes 12582912 | tf_op jit(solution)/shard_map/all_to_all | solution.py:199
  562.0 469.1 %reduce-scatter.3.cloned.1.call-start = ((), (), s32[]{:S(2)}) async-start(), calls=%async_computation.14 | async-start | bytes 10485760 | tf_op jit(solution)/shard_map/reduce_scatter | solution.py:268
  692.4 212.4 %all-to-all-start.5 = ((bf16[8,3,6,64,1024]{4,3,2,1,0:T(8,128)(2,1)}), bf16[8,3,6,64,1024]{4,3,2,1,0:T(8,128)(2,1)}, u32[]{:S(2)}, u32[]{:S(2)}) async-start(bf16[8,3,6,64,1024]{4,3,2,1,0:T(8,128)(2,1)} %get-tuple-element.77), calls=%async_computation.5 | async-start | bytes 37748736 | tf_op jit(solution)/shard_map/all_to_all | solution.py:199
  698.4 335.5 %reduce-scatter.5.cloned.1.call-start = ((), (), s32[]{:S(2)}) async-start(), calls=%async_computation.15 | async-start | bytes 10485760 | tf_op jit(solution)/shard_map/reduce_scatter | solution.py:269
  698.4 4.3 copy-start.1
  911.9 76.3 %all-to-all-start.7 = ((bf16[8,1,6,64,1024]{4,3,2,1,0:T(8,128)(2,1)}), bf16[8,1,6,64,1024]{4,3,2,1,0:T(8,128)(2,1)}, u32[]{:S(2)}, u32[]{:S(2)}) async-start(bf16[8,1,6,64,1024]{4,3,2,1,0:T(8,128)(2,1)} %get-tuple-element.81), calls=%async_computation.7 | async-start | bytes 12582912 | tf_op jit(solution)/shard_map/all_to_all | solution.py:199
  916.9 4.5 copy-start.3
  916.9 10.8 copy-start.14
  916.9 11.0 %copy-start.7 = (s32[6,1024]{1,0:T(8,128)S(1)}, s32[6,1024]{1,0:T(8,128)}, u32[]{:S(2)}) copy-start(s32[6,1024]{1,0:T(8,128)} %param.19) | copy-start | bytes 73732
  916.9 11.0 %copy-start.13 = (s32[6,1024]{1,0:T(8,128)S(1)}, s32[6,1024]{1,0:T(8,128)}, u32[]{:S(2)}) copy-start(s32[6,1024]{1,0:T(8,128)} %copy-done.12) | copy-start | bytes 73732
  919.1 9.8 copy-start.9
  919.1 9.9 copy-start.11
  919.1 9.9 copy-start.15
  929.5 7.1 copy-start
  988.2 48.3 %all-to-all-start.8 = ((f32[32,16,128]{2,1,0:T(8,128)}), f32[32,16,128]{2,1,0:T(8,128)S(1)}, u32[]{:S(2)}, u32[]{:S(2)}) async-start(f32[32,16,128]{2,1,0:T(8,128)} %pad_maximum_fusion), calls=%async_computation.8 | async-start | bytes 524288 | tf_op jit(solution)/shard_map/all_to_all | solution.py:297
  1037.3 39.0 %all-to-all-start.9 = ((f32[32,8,128]{2,1,0:T(8,128)}), f32[32,8,128]{2,1,0:T(8,128)S(1)}, u32[]{:S(2)}, u32[]{:S(2)}) async-start(f32[32,8,128]{2,1,0:T(8,128)} %broadcast_in_dim.81), calls=%async_computation.11 | async-start | bytes 262144 | tf_op jit(solution)/shard_map/all_to_all | solution.py:299
Sparse Core Ops, SparseCore 0:
  276.8 80.0 all-gather.2
  358.4 79.2 all-gather.4
  692.5 143.7 reduce-scatter.2
  838.5 145.1 reduce-scatter.4
